TPU v7x, 32 devices: a whole 2x2x4 slice. The times are simulated.
32 devices in a mesh: row: 8 (over z, core), col: 4 (over y, x).
Axes of the slice: x: 2, y: 2, z: 4, core: 2. Of those that a mesh axis runs over, the one named last changes fastest.
Arguments:
- inverse_tiles: bfloat16 [12288, 12288], P('row', 'col'), may hold values from -6 to 6
- factor: bfloat16 [12288, 2048], P('row', 'col'), may hold values from -0.0546875 to 0.0546875
- block_mask: int32 [96, 16], replicated, may hold values 0 or 1
- diag_inverse: float32 [16, 128, 128], replicated, may hold values from -6 to 6
Outputs:
- off_block: bfloat16 [2048, 12288], P('col', 'row')
- diag_block: float32 [16, 128, 128], P('col')
All inputs are finite; a program needn't handle non-finite values.
Results may differ from a plain program's by a relative error of at most 0.012.
Values may be sent and summed in bfloat16 or wider, within the bound.
No kernel may reach another device: no remote copies, remote signals or barrier semaphores. Data moves between devices by JAX's collectives and lax.ppermute only.
A program may use at most 128 MiB of HBM per device.

v0:
```python
import jax
import jax.numpy as jnp
from jax import lax
from jax.sharding import PartitionSpec as P


def from_root(value, axis, source):
    kept = jnp.where(lax.axis_index(axis) == source, value, 0).astype(value.dtype)
    return lax.psum(kept, axis)


def per_device(inverse_tiles, factor, block_mask, diag_inverse):
    rows_here, cols_here = factor.shape
    block_width = diag_inverse.shape[1]
    sup_here = cols_here // block_width
    blocks_here = rows_here // block_width
    row_index = lax.axis_index("row")
    col_index = lax.axis_index("col")
    mask_here = lax.dynamic_slice(
        block_mask, (row_index * blocks_here, col_index * sup_here), (blocks_here, sup_here)
    )
    keep_mask = jnp.repeat(jnp.repeat(mask_here, block_width, 0), block_width, 1).astype(
        jnp.bfloat16
    )
    masked = factor * keep_mask
    full_rows = lax.all_gather(masked, "col", axis=1, tiled=True)
    row_ratio = lax.axis_size("row") // lax.axis_size("col")
    row_pieces = []
    for offset in range(row_ratio):
        row_pieces.append(from_root(full_rows, "row", row_ratio * col_index + offset))
    summed = jnp.zeros((full_rows.shape[1], rows_here), jnp.float32)
    for offset in range(row_ratio):
        columns = row_pieces[offset]
        inverse_part = inverse_tiles[:, offset * rows_here : (offset + 1) * rows_here]
        summed = summed + lax.dot_general(
            columns, inverse_part, (((0,), (1,)), ((), ())), preferred_element_type=jnp.float32
        )
    reduced = lax.psum_scatter(summed, "col", scatter_dimension=0, tiled=True)
    left_factor = masked.astype(jnp.float32).reshape(rows_here, sup_here, block_width)
    right_product = reduced.reshape(sup_here, block_width, rows_here)
    partial_diag = jnp.einsum(
        "jbr,rja->jab", right_product, left_factor, precision=lax.Precision.HIGHEST
    )
    summed_diag = lax.psum(partial_diag.astype(jnp.bfloat16), "row").astype(jnp.float32)
    own_diag = lax.dynamic_slice_in_dim(diag_inverse, col_index * sup_here, sup_here, 0)
    return ((-reduced).astype(jnp.bfloat16), own_diag + summed_diag)


def solution(mesh):
    return jax.shard_map(
        per_device,
        mesh=mesh,
        in_specs=(P("row", "col"), P("row", "col"), P(), P()),
        out_specs=(P("col", "row"), P("col", None, None)),
        check_vma=False,
    )
```

profile of v0, /device:TPU:0, one launch (start us, length us, event | category | flops | bytes accessed | tf_op | source)
XLA Modules:
  0.0 571.0 jit_solution(12963636259537801392)
XLA Ops:
  7.2 0.0 all-gather.2.cloned.1.call-start
  7.2 0.8 dynamic-slice_convert_fusion
  8.0 0.1 copy.6
  8.1 0.1 broadcast_in_dim.11
  8.2 1.9 broadcast_in_dim.12
  10.1 2.8 bitcast_multiply_fusion
  12.9 0.0 all-gather.2.cloned.1.call-update
  12.9 0.0 all-reduce.6.cloned.1.call-start
  12.9 72.7 %all-gather.2.cloned.1.call-done = bf16[1536,2048]{1,0:T(8,128)(2,1)} async-done(((bf16[1536,512]{1,0:T(8,128)(2,1)}), bf16[1536,2048]{1,0:T(8,128)(2,1)}) %all-gather.2.cloned.1.call-update) | async-done | bytes 6291472 | tf_op jit(solution)/shard_map/all_gather | solution.py:26
  85.7 8.1 %broadcast_select_fusion = (bf16[1536,2048]{1,0:T(8,128)(2,1)}, bf16[1536,2048]{1,0:T(8,128)(2,1)}) fusion(bf16[1536,2048]{1,0:T(8,128)(2,1)} %all-gather.2.cloned.1.call-done, pred[]{:T(512)S(6)} %eq.7, pred[]{:T(512)S(6)} %eq.6), kind=kLoop, calls=%fused_computation.1 | loop fusion | flops 6291456 | bytes 18874370 | tf_op jit(solution)/shard_map/jit(_where)/select_n | solution.py:8
  93.8 0.0 slice-start
  93.8 0.0 all-reduce.6.cloned.1.call-update
  93.8 0.0 reduce-scatter.2.cloned.1.call-start
  93.9 254.7 %all-reduce.6.cloned.1.call-done = (bf16[1536,2048]{1,0:T(8,128)(2,1)}, bf16[1536,2048]{1,0:T(8,128)(2,1)}) async-done(((bf16[1536,2048]{1,0:T(8,128)(2,1)}, bf16[1536,2048]{1,0:T(8,128)(2,1)}), (bf16[1536,2048]{1,0:T(8,128)(2,1)}, bf16[1536,2048]{1,0:T(8,128)(2,1)})) %all-reduce.6.cloned.1.call-update) | async-done | bytes 12582928 | tf_op jit(solution)/shard_map/psum | solution.py:9
  348.6 0.0 slice-start.1
  348.6 0.0 slice-start.2
  348.6 16.3 %fusion.1 = f32[2048,1536]{1,0:T(8,128)} fusion(bf16[1536,2048]{1,0:T(8,128)(2,1)} %get-tuple-element.2, bf16[1536,3072]{1,0:T(8,128)(2,1)} %param.4), kind=kOutput, calls=%fused_computation.4 | convolution fusion | flops 9663676416 | bytes 23592960 | tf_op jit(solution)/shard_map/dot_general | solution.py:35
  364.8 0.0 slice-done
  364.9 0.0 slice-done.1
  364.9 0.0 slice-done.2
  364.9 16.9 %convolution_add_fusion = f32[2048,1536]{1,0:T(8,128)} fusion(f32[2048,1536]{1,0:T(8,128)} %fusion.1, bf16[1536,2048]{1,0:T(8,128)(2,1)} %get-tuple-element.3, bf16[1536,3072]{1,0:T(8,128)(2,1)S(1)} %bitcast.15), kind=kOutput, calls=%fused_computation | convolution fusion | flops 9666822144 | bytes 36175872 | tf_op jit(solution)/shard_map/dot_general | solution.py:35
  381.8 0.0 copy-start
  381.8 0.0 reduce-scatter.2.cloned.1.call-update
  381.8 0.2 all-reduce.4.cloned.1.call-start
  382.1 1.2 copy-done
  383.2 1.6 copy.8
  384.8 118.0 %reduce-scatter.2.cloned.1.call-done = f32[512,1536]{1,0:T(8,128)} async-done(((f32[2048,1536]{1,0:T(8,128)}), f32[512,1536]{1,0:T(8,128)}) %reduce-scatter.2.cloned.1.call-update) | async-done | bytes 3145744 | tf_op jit(solution)/shard_map/reduce_scatter | solution.py:38
  502.7 0.0 copy-start.1
  502.7 4.8 convolution_convert_fusion
  507.6 0.0 all-reduce.4.cloned.1.call-update
  507.6 0.0 copy-done.1
  507.6 1.5 negate_convert_fusion
  509.1 53.6 %all-reduce.4.cloned.1.call-done = bf16[4,128,128]{2,1,0:T(8,128)(2,1)} async-done(((bf16[4,128,128]{2,1,0:T(8,128)(2,1)}), bf16[4,128,128]{2,1,0:T(8,128)(2,1)}) %all-reduce.4.cloned.1.call-update) | async-done | bytes 131088 | tf_op jit(solution)/shard_map/psum | solution.py:44
  562.7 1.7 convert_add_fusion
  (1 shorter events, 0.0 us)
Async XLA Ops:
  7.2 78.5 %all-gather.2.cloned.1.call-start = ((), (), s32[]{:S(2)}) async-start(), calls=%async_computation.1 | async-start | bytes 7864320 | tf_op jit(solution)/shard_map/all_gather | solution.py:26
  12.9 335.7 %all-reduce.6.cloned.1.call-start = ((), (), s32[]{:S(2)}) async-start(), calls=%async_computation.4 | async-start | bytes 25165824 | tf_op jit(solution)/shard_map/psum | solution.py:9
  93.8 271.1 %slice-start = ((s8[9437184]{0:T(1024)(128)(4,1)}), s8[1048576]{0:T(1024)(128)(4,1)S(1)}, s32[]{:S(2)}) async-start(s8[9437184]{0:T(1024)(128)(4,1)} %bitcast.14), calls=%async_computation.5 | async-start | bytes 2097152
  93.8 408.9 %reduce-scatter.2.cloned.1.call-start = ((), (), s32[]{:S(2)}) async-start(), calls=%async_computation.2 | async-start | bytes 15728640 | tf_op jit(solution)/shard_map/reduce_scatter | solution.py:38
  348.6 16.3 %slice-start.1 = ((s8[9437184]{0:T(1024)(128)(4,1)}), s8[4194304]{0:T(1024)(128)(4,1)S(1)}, s32[]{:S(2)}) async-start(s8[9437184]{0:T(1024)(128)(4,1)} %bitcast.14), calls=%async_computation.6 | async-start | bytes 8388608
  348.6 16.3 %slice-start.2 = ((s8[9437184]{0:T(1024)(128)(4,1)}), s8[4194304]{0:T(1024)(128)(4,1)S(1)}, s32[]{:S(2)}) async-start(s8[9437184]{0:T(1024)(128)(4,1)} %bitcast.14), calls=%async_computation.7 | async-start | bytes 8388608
  381.8 1.4 copy-start
  381.8 180.9 %all-reduce.4.cloned.1.call-start = ((), (), s32[]{:S(2)}) async-start(), calls=%async_computation.3 | async-start | bytes 262144 | tf_op jit(solution)/shard_map/psum | solution.py:44
  502.7 4.9 copy-start.1
Sparse Core Ops, SparseCore 0:
  13.0 72.6 all-gather.1
  93.9 254.5 all-reduce.5
  381.9 120.7 reduce-scatter.1
  507.7 54.9 all-reduce.3
where the time goes:
time: 571 us
  waiting for transfers between devices  499 us (87%)
  matrix products  38 us (7%)
  other arithmetic  14.9 us (3%)
  between operations  13.8 us (2%)
    psum x1, waiting for transfers between devices, from_root(): return lax.psum(kept, axis)  255 us
    reduce_scatter x1, waiting for transfers between devices, per_device(): reduced = lax.psum_scatter(summed, 'col', scatter_dimension=0, tiled=True)  118 us
    all_gather x1, waiting for transfers between devices, per_device(): full_rows = lax.all_gather(masked, 'col', axis=1, tiled=True)  72.7 us
    psum x1, waiting for transfers between devices, per_device(): lax.psum(partial_diag.astype(jnp.bfloat16), 'row').astype(jnp.float32)  53.6 us
    dot_general x2, matrix products, per_device(): lax.dot_general(columns, inverse_part, (((0,), (1,)), ((), ())), preferre...  33.2 us
  transfers between devices with their start and end apart: 4, of which 4 were waited for; matrix products, arithmetic and copies ran while one was open for 1% of the time, Pallas kernels for 0%

commit v1 on v0

--- a/solution.py
+++ b/solution.py
@@ -6,7 +6,7 @@
 
 def from_root(value, axis, source):
     kept = jnp.where(lax.axis_index(axis) == source, value, 0).astype(value.dtype)
-    return lax.psum(kept, axis)
+    return jnp.sum(lax.all_gather(kept, axis), axis=0)
 
 
 def per_device(inverse_tiles, factor, block_mask, diag_inverse):

time: 571 us -> 1190 us (2.08)
  waiting for transfers between devices: 499 us -> 1070 us
  other arithmetic: 14.9 us -> 62.9 us
    all_gather x0 -> x2, waiting for transfers between devices: none -> 826 us  [from_root(): return jnp.sum(lax.all_gather(kept, axis), axis=0)]
    psum x1 -> x0, waiting for transfers between devices: 255 us -> none  [from_root(): return lax.psum(kept, axis)]
    reduce_sum x0 -> x2, other arithmetic: none -> 48.1 us  [from_root(): return jnp.sum(lax.all_gather(kept, axis), axis=0)]
  transfers between devices with their start and end apart: 4 -> 5, of which waited for: 4 -> 5; matrix products, arithmetic and copies ran while one was open for 1% -> 3% of each run, Pallas kernels for 0% -> 0%
where the time goes in v1:
time: 1190 us
  waiting for transfers between devices  1070 us (90%)
  other arithmetic  62.9 us (5%)
  matrix products  37.2 us (3%)
  between operations  13.8 us (1%)
    all_gather x2, waiting for transfers between devices, from_root(): return jnp.sum(lax.all_gather(kept, axis), axis=0)  826 us
    reduce_scatter x1, waiting for transfers between devices, per_device(): reduced = lax.psum_scatter(summed, 'col', scatter_dimension=0, tiled=True)  116 us
    all_gather x1, waiting for transfers between devices, per_device(): full_rows = lax.all_gather(masked, 'col', axis=1, tiled=True)  72.7 us
    psum x1, waiting for transfers between devices, per_device(): lax.psum(partial_diag.astype(jnp.bfloat16), 'row').astype(jnp.float32)  53.6 us
    reduce_sum x2, other arithmetic, from_root(): return jnp.sum(lax.all_gather(kept, axis), axis=0)  48.1 us
    dot_general x2, matrix products, per_device(): lax.dot_general(columns, inverse_part, (((0,), (1,)), ((), ())), preferre...  32.4 us
  transfers between devices with their start and end apart: 5, of which 5 were waited for; matrix products, arithmetic and copies ran while one was open for 3% of the time, Pallas kernels for 0%

profile of v1, /device:TPU:0, one launch (start us, length us, event | category | flops | bytes accessed | tf_op | source)
XLA Modules:
  0.0 1188.2 jit_solution(15474356219883665549)
XLA Ops:
  7.2 0.0 all-gather.6.cloned.1.call-start
  7.2 0.8 dynamic-slice_convert_fusion
  8.0 0.1 copy.6
  8.1 0.1 broadcast_in_dim.11
  8.2 1.9 broadcast_in_dim.12
  10.1 2.8 bitcast_multiply_fusion
  12.9 0.0 all-gather.6.cloned.1.call-update
  12.9 0.0 all-gather.10.cloned.1.call-start
  12.9 72.7 %all-gather.6.cloned.1.call-done = bf16[1536,2048]{1,0:T(8,128)(2,1)} async-done(((bf16[1536,512]{1,0:T(8,128)(2,1)}), bf16[1536,2048]{1,0:T(8,128)(2,1)}) %all-gather.6.cloned.1.call-update) | async-done | bytes 6291472 | tf_op jit(solution)/shard_map/all_gather | solution.py:26
  85.7 8.1 broadcast_select_fusion
  93.7 0.0 all-gather.10.cloned.1.call-update
  93.8 0.0 all-gather.8.cloned.1.call-start
  93.8 0.7 all-gather.8.cloned.1.call-update
  94.5 0.0 reduce-scatter.2.cloned.1.call-start
  94.5 426.7 %all-gather.10.cloned.1.call-done = bf16[12288,2048]{1,0:T(8,128)(2,1)} async-done(((bf16[1536,2048]{1,0:T(8,128)(2,1)}), bf16[12288,2048]{1,0:T(8,128)(2,1)}) %all-gather.10.cloned.1.call-update) | async-done | bytes 50331664 | tf_op jit(solution)/shard_map/all_gather | solution.py:9
  521.3 28.1 %reduce_sum.25 = bf16[1536,2048]{1,0:T(8,128)(2,1)} reduce(bf16[8,1536,2048]{2,1,0:T(8,128)(2,1)} %bitcast.12, bf16[]{:T(256)} %constant.26.clone.1), dimensions={0}, to_apply=%region_1.2 | reduce | flops 22020096 | bytes 56623104 | tf_op jit(solution)/shard_map/reduce_sum | solution.py:9
  549.4 399.2 %all-gather.8.cloned.1.call-done = bf16[12288,2048]{1,0:T(8,128)(2,1)} async-done(((bf16[1536,2048]{1,0:T(8,128)(2,1)}), bf16[12288,2048]{1,0:T(8,128)(2,1)}) %all-gather.8.cloned.1.call-update) | async-done | bytes 50331664 | tf_op jit(solution)/shard_map/all_gather | solution.py:9
  948.5 0.0 slice-start
  948.5 20.0 %reduce_sum.24 = bf16[1536,2048]{1,0:T(8,128)(2,1)} reduce(bf16[8,1536,2048]{2,1,0:T(8,128)(2,1)} %bitcast.13, bf16[]{:T(256)} %constant.26.clone.1), dimensions={0}, to_apply=%region_0.1 | reduce | flops 22020096 | bytes 56623104 | tf_op jit(solution)/shard_map/reduce_sum | solution.py:9
  968.6 0.0 slice-start.1
  968.6 16.3 %fusion.1 = f32[2048,1536]{1,0:T(8,128)} fusion(bf16[1536,2048]{1,0:T(8,128)(2,1)} %reduce_sum.24, bf16[1536,3072]{1,0:T(8,128)(2,1)} %param.4), kind=kOutput, calls=%fused_computation.4 | convolution fusion | flops 9663676416 | bytes 23592960 | tf_op jit(solution)/shard_map/dot_general | solution.py:35
  984.9 0.0 slice-done
  984.9 0.0 slice-done.1
  984.9 16.1 %convolution_add_fusion = f32[2048,1536]{1,0:T(8,128)} fusion(f32[2048,1536]{1,0:T(8,128)} %fusion.1, bf16[1536,2048]{1,0:T(8,128)(2,1)S(1)} %bitcast.18, bf16[1536,3072]{1,0:T(8,128)(2,1)} %param.4), kind=kOutput, calls=%fused_computation | convolution fusion | flops 9666822144 | bytes 36175872 | tf_op jit(solution)/shard_map/dot_general | solution.py:35
  1001.0 0.0 copy-start
  1001.0 0.0 reduce-scatter.2.cloned.1.call-update
  1001.0 0.2 all-reduce.2.cloned.1.call-start
  1001.2 1.2 copy-done
  1002.4 1.6 copy.8
  1003.9 116.0 %reduce-scatter.2.cloned.1.call-done = f32[512,1536]{1,0:T(8,128)} async-done(((f32[2048,1536]{1,0:T(8,128)}), f32[512,1536]{1,0:T(8,128)}) %reduce-scatter.2.cloned.1.call-update) | async-done | bytes 3145744 | tf_op jit(solution)/shard_map/reduce_scatter | solution.py:38
  1119.9 0.0 copy-start.1
  1119.9 4.8 convolution_convert_fusion
  1124.8 0.0 all-reduce.2.cloned.1.call-update
  1124.8 0.0 copy-done.1
  1124.8 1.5 negate_convert_fusion
  1126.3 53.6 %all-reduce.2.cloned.1.call-done = bf16[4,128,128]{2,1,0:T(8,128)(2,1)} async-done(((bf16[4,128,128]{2,1,0:T(8,128)(2,1)}), bf16[4,128,128]{2,1,0:T(8,128)(2,1)}) %all-reduce.2.cloned.1.call-update) | async-done | bytes 131088 | tf_op jit(solution)/shard_map/psum | solution.py:44
  1179.9 1.7 convert_add_fusion
  (1 shorter events, 0.0 us)
Async XLA Ops:
  7.2 78.5 %all-gather.6.cloned.1.call-start = ((), (), s32[]{:S(2)}) async-start(), calls=%async_computation.1 | async-start | bytes 7864320 | tf_op jit(solution)/shard_map/all_gather | solution.py:26
  12.9 508.4 %all-gather.10.cloned.1.call-start = ((), (), s32[]{:S(2)}) async-start(), calls=%async_computation.5 | async-start | bytes 56623104 | tf_op jit(solution)/shard_map/all_gather | solution.py:9
  93.8 854.8 %all-gather.8.cloned.1.call-start = ((), (), s32[]{:S(2)}) async-start(), calls=%async_computation.4 | async-start | bytes 56623104 | tf_op jit(solution)/shard_map/all_gather | solution.py:9
  94.5 1025.4 %reduce-scatter.2.cloned.1.call-start = ((), (), s32[]{:S(2)}) async-start(), calls=%async_computation.2 | async-start | bytes 15728640 | tf_op jit(solution)/shard_map/reduce_scatter | solution.py:38
  948.5 36.3 %slice-start = ((s8[6291456]{0:T(1024)(128)(4,1)}), s8[2097152]{0:T(1024)(128)(4,1)S(1)}, s32[]{:S(2)}) async-start(s8[6291456]{0:T(1024)(128)(4,1)} %bitcast.17), calls=%async_computation.6 | async-start | bytes 4194304
  968.6 16.3 %slice-start.1 = ((s8[6291456]{0:T(1024)(128)(4,1)}), s8[4194304]{0:T(1024)(128)(4,1)S(1)}, s32[]{:S(2)}) async-start(s8[6291456]{0:T(1024)(128)(4,1)} %bitcast.17), calls=%async_computation.7 | async-start | bytes 8388608
  1001.0 1.4 copy-start
  1001.0 178.9 %all-reduce.2.cloned.1.call-start = ((), (), s32[]{:S(2)}) async-start(), calls=%async_computation.3 | async-start | bytes 262144 | tf_op jit(solution)/shard_map/psum | solution.py:44
  1119.9 4.9 copy-start.1
Sparse Core Ops, SparseCore 0:
  13.0 72.6 all-gather.5
  93.9 427.3 all-gather.9
  522.9 425.5 all-gather.7
  1001.1 118.7 reduce-scatter.1
  1124.9 54.9 all-reduce.1
